TPU v7x, 32 devices: a whole 2x2x4 slice. The times are simulated.
32 devices in a mesh: pair: 4 (over y, core), aux: 8 (over z, x).
Axes of the slice: x: 2, y: 2, z: 4, core: 2. Of those that a mesh axis runs over, the one named last changes fastest.
Arguments:
- occupied_index: int32 [4], P('pair'), may hold values from 0 to 3
- doubles_slab: bfloat16 [4, 2048, 2048], P('pair', 'aux'), may hold values from -0.09375 to 0.09375
- lambda_slab: bfloat16 [4, 2048, 2048], P('pair', 'aux'), may hold values from -0.09375 to 0.09375
- aux_factors: bfloat16 [4, 8, 2048], P('pair'), may hold values from -6 to 6
- dressed_factors: bfloat16 [4, 8, 2048], P('pair'), may hold values from -6 to 6
- virtual_coefs: bfloat16 [1024, 2048], P(None, 'aux'), may hold values from -0.125 to 0.125
- occupied_coefs: float32 [512, 4], replicated, may hold values from -3 to 3
Outputs:
- gamma_basis: bfloat16 [8, 512, 1024], P('pair', None, 'aux')
Inputs may be any that keep to these rules, and one draw needn't show every extreme that they name: `occupied_index`: entry p is the occupied index i that forms a pair with the occupied index j = p.
All inputs are finite; a program needn't handle non-finite values.
Results may differ from a plain program's by a relative error of at most 0.014.
Values may be sent and summed in bfloat16 or wider, within the bound.
No kernel may reach another device: no remote copies, remote signals or barrier semaphores. Data moves between devices by JAX's collectives and lax.ppermute only.
A program may use at most 64 MiB of HBM per device.

v0:
```python
import jax
import jax.numpy as jnp
from jax import lax
from jax.sharding import PartitionSpec as P

I_WIN = 4


def shards(
    occupied_index,
    doubles_slab,
    lambda_slab,
    aux_factors,
    dressed_factors,
    virtual_coefs,
    occupied_coefs,
):
    first_amps = doubles_slab[0]
    second_amps = lambda_slab[0]
    factor_one = aux_factors[0]
    factor_two = dressed_factors[0]
    contract = (((1,), (1,)), ((), ()))
    groups = lax.axis_size("pair")
    product = lax.dot_general(factor_one, first_amps, contract, preferred_element_type=jnp.float32)
    product = product + lax.dot_general(
        factor_two, second_amps, contract, preferred_element_type=jnp.float32
    )
    grouped = product.reshape(groups, product.shape[0] // groups, product.shape[1])
    index_column = jnp.broadcast_to(occupied_index[0].astype(jnp.float32), (groups, 1))
    received, sender_index = (
        lax.all_to_all(grouped, "pair", split_axis=0, concat_axis=0, tiled=True),
        lax.all_to_all(index_column, "pair", split_axis=0, concat_axis=0, tiled=True),
    )
    levels = jnp.arange(I_WIN).astype(jnp.float32)
    onehot = (sender_index[:, 0][:, None] == levels[None, :]).astype(jnp.float32)
    summed = jnp.einsum("pi,pqa->qia", onehot, received, precision=lax.Precision.HIGHEST)
    gamma_mo = summed.astype(jnp.bfloat16)
    virtual_term = jnp.einsum(
        "qia,na->qin", gamma_mo, virtual_coefs, preferred_element_type=jnp.float32
    )
    half_back = lax.psum_scatter(
        virtual_term.astype(jnp.bfloat16), "aux", scatter_dimension=2, tiled=True
    ).astype(jnp.float32)
    gamma_basis = jnp.einsum(
        "mi,qin->qmn", occupied_coefs, half_back, precision=lax.Precision.HIGHEST
    )
    return gamma_basis.astype(jnp.bfloat16)


def solution(mesh):
    placed = (
        P("pair"),
        P("pair", "aux", None),
        P("pair", "aux", None),
        P("pair", None, None),
        P("pair", None, None),
        P(None, "aux"),
        P(),
    )
    return jax.shard_map(
        shards, mesh=mesh, in_specs=placed, out_specs=P("pair", None, "aux"), check_vma=False
    )
```

profile of v0, /device:TPU:0, one launch (start us, length us, event | category | flops | bytes accessed | tf_op | source)
XLA Modules:
  0.0 97.2 jit_solution(9885967186416020520)
XLA Ops:
  6.5 0.0 copy-start
  6.5 0.0 copy-start.1
  7.3 0.6 broadcast_in_dim.4
  7.9 4.3 %all-to-all-start.1 = ((f32[4,1,1]{2,1,0:T(1,128)}), f32[4,1,1]{2,1,0:T(1,128)S(1)}, u32[]{:S(2)}, u32[]{:S(2)}) async-start(f32[4,1,1]{2,1,0:T(1,128)} %broadcast_in_dim.4), calls=%async_computation.1 | async-start | bytes 4096 | tf_op jit(solution)/shard_map/all_to_all | solution.py:32
  12.2 0.0 copy-done
  12.2 0.0 copy-start.3
  12.2 1.1 %fusion.3 = f32[8,256]{1,0:T(8,128)S(1)} fusion(bf16[1,256,2048]{2,1,0:T(8,128)(2,1)S(1)} %copy-done, bf16[1,8,2048]{2,1,0:T(8,128)(2,1)} %param.10), kind=kOutput, calls=%fused_computation.7 | convolution fusion | flops 8388608 | bytes 1089536 | tf_op jit(solution)/shard_map/dot_general | solution.py:24
  13.3 0.0 copy-done.1
  13.3 0.0 copy-done.3
  13.4 0.0 copy-start.2
  13.4 0.4 convolution_add_fusion
  13.7 0.6 reshape.11
  14.4 1.6 %all-to-all-done.1 = f32[4,1,1]{2,1,0:T(1,128)S(1)} async-done(((f32[4,1,1]{2,1,0:T(1,128)}), f32[4,1,1]{2,1,0:T(1,128)S(1)}, u32[]{:S(2)}, u32[]{:S(2)}) %all-to-all-start.1) | async-done | bytes 48 | tf_op jit(solution)/shard_map/all_to_all | solution.py:32
  16.0 3.2 %all-to-all-start = ((f32[4,2,256]{2,1,0:T(2,128)}), f32[4,2,256]{2,1,0:T(2,128)S(1)}, u32[]{:S(2)}, u32[]{:S(2)}) async-start(f32[4,2,256]{2,1,0:T(2,128)} %reshape.11), calls=%async_computation | async-start | bytes 16384 | tf_op jit(solution)/shard_map/all_to_all | solution.py:31
  19.2 0.0 reduce-scatter.4.cloned.1.call-start
  19.3 0.1 reduce
  19.4 3.6 %all-to-all-done = f32[4,2,256]{2,1,0:T(2,128)S(1)} async-done(((f32[4,2,256]{2,1,0:T(2,128)}), f32[4,2,256]{2,1,0:T(2,128)S(1)}, u32[]{:S(2)}, u32[]{:S(2)}) %all-to-all-start) | async-done | bytes 8224 | tf_op jit(solution)/shard_map/all_to_all | solution.py:31
  23.0 0.2 fusion.1
  23.2 0.0 copy-done.2
  23.2 0.2 convolution_convert_fusion.1
  23.5 0.5 copy.14
  23.9 1.0 reshape.15
  24.9 0.0 reduce-scatter.4.cloned.1.call-update
  24.9 0.0 copy-start.4
  24.9 63.3 %reduce-scatter.4.cloned.1.call-done = bf16[128,8]{1,0:T(8,128)(2,1)} async-done(((bf16[1024,8]{1,0:T(8,128)(2,1)}), bf16[128,8]{1,0:T(8,128)(2,1)}) %reduce-scatter.4.cloned.1.call-update) | async-done | bytes 2064
  88.3 0.8 reshape.16
  89.1 0.0 copy-done.4
  89.1 0.3 fusion
  89.5 0.8 copy.13
  (1 shorter events, 0.0 us)
Async XLA Ops:
  6.5 5.7 %copy-start = (bf16[1,256,2048]{2,1,0:T(8,128)(2,1)S(1)}, bf16[1,256,2048]{2,1,0:T(8,128)(2,1)}, u32[]{:S(2)}) copy-start(bf16[1,256,2048]{2,1,0:T(8,128)(2,1)} %param.8) | copy-start | bytes 3145732
  6.5 6.8 %copy-start.1 = (bf16[1,256,2048]{2,1,0:T(8,128)(2,1)S(1)}, bf16[1,256,2048]{2,1,0:T(8,128)(2,1)}, u32[]{:S(2)}) copy-start(bf16[1,256,2048]{2,1,0:T(8,128)(2,1)} %param.9) | copy-start | bytes 3145732
  7.9 8.0 %all-to-all-start.1 = ((f32[4,1,1]{2,1,0:T(1,128)}), f32[4,1,1]{2,1,0:T(1,128)S(1)}, u32[]{:S(2)}, u32[]{:S(2)}) async-start(f32[4,1,1]{2,1,0:T(1,128)} %broadcast_in_dim.4), calls=%async_computation.1 | async-start | bytes 4096 | tf_op jit(solution)/shard_map/all_to_all | solution.py:32
  12.2 1.1 %copy-start.3 = (bf16[1,8,2048]{2,1,0:T(8,128)(2,1)S(1)}, bf16[1,8,2048]{2,1,0:T(8,128)(2,1)}, u32[]{:S(2)}) copy-start(bf16[1,8,2048]{2,1,0:T(8,128)(2,1)} %param.11) | copy-start | bytes 98308
  13.4 9.9 %copy-start.2 = (bf16[1024,256]{1,0:T(8,128)(2,1)S(1)}, bf16[1024,256]{1,0:T(8,128)(2,1)}, u32[]{:S(2)}) copy-start(bf16[1024,256]{1,0:T(8,128)(2,1)} %param.12) | copy-start | bytes 1572868
  16.0 7.0 %all-to-all-start = ((f32[4,2,256]{2,1,0:T(2,128)}), f32[4,2,256]{2,1,0:T(2,128)S(1)}, u32[]{:S(2)}, u32[]{:S(2)}) async-start(f32[4,2,256]{2,1,0:T(2,128)} %reshape.11), calls=%async_computation | async-start | bytes 16384 | tf_op jit(solution)/shard_map/all_to_all | solution.py:31
  19.2 69.0 %reduce-scatter.4.cloned.1.call-start = ((), (), s32[]{:S(2)}) async-start(), calls=%async_computation.3 | async-start | bytes 294912
  24.9 64.2 %copy-start.4 = (f32[512,4]{0,1:T(4,128)S(1)}, f32[512,4]{0,1:T(4,128)}, u32[]{:S(2)}) copy-start(f32[512,4]{0,1:T(4,128)} %param.13) | copy-start | bytes 24580
Sparse Core Ops, SparseCore 0:
  25.0 63.1 reduce-scatter.3
where the time goes:
time: 97.5 us; the launch traced here: 97.2 us
  waiting for transfers between devices  68.6 us (70%)
  between operations  14.3 us (15%)
  starting transfers between devices  7.56 us (8%)
  local copies, waits for them, and re-layouts  4.37 us (4%)
  matrix products  2.27 us (2%)
    unnamed x2, waiting for transfers between devices  63.4 us
    all_to_all x1, starting transfers between devices, shards(): lax.all_to_all(index_column, 'pair', split_axis=0, concat_axis=0, tiled=T...  4.26 us
    all_to_all x1, waiting for transfers between devices, shards(): lax.all_to_all(grouped, 'pair', split_axis=0, concat_axis=0, tiled=True)  3.6 us
    all_to_all x1, starting transfers between devices, shards(): lax.all_to_all(grouped, 'pair', split_axis=0, concat_axis=0, tiled=True)  3.25 us
    unnamed x13, local copies, waits for them, and re-layouts  2.3 us
  transfers between devices with their start and end apart: 3, of which 3 were waited for; matrix products, arithmetic and copies ran while one was open for 2% of the time, Pallas kernels for 0%

commit v1 on v0

v1 whole, which is shorter than its diff:
```python
import jax
import jax.numpy as jnp
from jax import lax
from jax.sharding import PartitionSpec as P


def shards(
    occupied_index,
    doubles_slab,
    lambda_slab,
    aux_factors,
    dressed_factors,
    virtual_coefs,
    occupied_coefs,
):
    contract = (((1,), (1,)), ((), ()))
    pairs = lax.axis_size("pair")
    blocks = lax.axis_size("aux")
    levels = occupied_coefs.shape[1]
    product = lax.dot_general(
        aux_factors[0], doubles_slab[0], contract, preferred_element_type=jnp.float32
    )
    product = product + lax.dot_general(
        dressed_factors[0], lambda_slab[0], contract, preferred_element_type=jnp.float32
    )
    half = lax.dot_general(
        product.astype(jnp.bfloat16), virtual_coefs, contract, preferred_element_type=jnp.float32
    )
    q_own = half.shape[0] // pairs
    nu_own = half.shape[1] // blocks
    cells = half.reshape(pairs, q_own, blocks, nu_own).transpose(0, 2, 1, 3)
    cells = cells.reshape(pairs * blocks, 1, q_own, nu_own)
    mine = jnp.arange(levels, dtype=jnp.int32) == occupied_index[0]
    cells = jnp.where(mine[None, :, None, None], cells, 0.0).astype(jnp.bfloat16)
    cells = cells.reshape(pairs * blocks, levels * q_own, nu_own)
    received = lax.all_to_all(cells, ("pair", "aux"), split_axis=0, concat_axis=0, tiled=True)
    summed = received.astype(jnp.float32).sum(axis=0).reshape(levels, q_own, nu_own)
    gamma_basis = sum(
        occupied_coefs[:, i][None, :, None] * summed[i][:, None, :] for i in range(levels)
    )
    return gamma_basis.astype(jnp.bfloat16)


def solution(mesh):
    placed = (
        P("pair"),
        P("pair", "aux", None),
        P("pair", "aux", None),
        P("pair", None, None),
        P("pair", None, None),
        P(None, "aux"),
        P(),
    )
    return jax.shard_map(
        shards, mesh=mesh, in_specs=placed, out_specs=P("pair", None, "aux"), check_vma=False
    )
```

time: 97.5 us -> 20.2 us (0.21)
  waiting for transfers between devices: 68.6 us -> 7.25 us
  between operations: 14.3 us -> 0.82 us
  local copies, waits for them, and re-layouts: 4.37 us -> 0.29 us
  other arithmetic: 0.12 us -> 1.8 us
    unnamed x2 -> x0, waiting for transfers between devices: 63.4 us -> none
    unnamed x13 -> x9, local copies, waits for them, and re-layouts: 2.3 us -> 0.04 us
    all_to_all x2 -> x1, waiting for transfers between devices: 5.21 us -> 7.25 us  [shards(): lax.all_to_all(cells, ('pair', 'aux'), split_axis=0, concat_axis=0, tiled...]
    convert_element_type x1 -> x2, other arithmetic: 0.01 us -> 1.75 us  [the longest x1 1.04 us: shards(): return gamma_basis.astype(jnp.bfloat16)]
    dot_general x5 -> x2, matrix products: 2.27 us -> 2.48 us  [the longest x1 1.67 us: shards(): lax.dot_general(aux_factors[0], doubles_slab[0], contract, preferred_elem...]
    all_to_all x2 -> x1, starting transfers between devices: 7.51 us -> 7.33 us  [shards(): lax.all_to_all(cells, ('pair', 'aux'), split_axis=0, concat_axis=0, tiled...]
  transfers between devices with their start and end apart: 3 -> 1, of which waited for: 3 -> 1; matrix products, arithmetic and copies ran while one was open for 2% -> 0% of each run, Pallas kernels for 0% -> 0%
where the time goes in v1:
time: 20.2 us; the launch traced here: 20 us
  starting transfers between devices  7.33 us (36%)
  waiting for transfers between devices  7.25 us (36%)
  matrix products  2.48 us (12%)
  other arithmetic  1.8 us (9%)
  between operations  0.82 us (4%)
  local copies, waits for them, and re-layouts  0.29 us (1%)
    all_to_all x1, starting transfers between devices, shards(): lax.all_to_all(cells, ('pair', 'aux'), split_axis=0, concat_axis=0, tiled...  7.33 us
    all_to_all x1, waiting for transfers between devices, shards(): lax.all_to_all(cells, ('pair', 'aux'), split_axis=0, concat_axis=0, tiled...  7.25 us
    dot_general x1, matrix products, shards(): lax.dot_general(aux_factors[0], doubles_slab[0], contract, preferred_elem...  1.67 us
    convert_element_type x1, other arithmetic, shards(): return gamma_basis.astype(jnp.bfloat16)  1.04 us
    dot_general x1, matrix products, shards(): lax.dot_general(product.astype(jnp.bfloat16), virtual_coefs, contract, pr...  0.81 us
    convert_element_type x1, other arithmetic, shards(): jnp.where(mine[None, :, None, None], cells, 0.0).astype(jnp.bfloat16)  0.71 us
  transfers between devices with their start and end apart: 1, of which 1 were waited for; matrix products, arithmetic and copies ran while one was open for 0% of the time, Pallas kernels for 0%

profile of v1, /device:TPU:0, one launch (start us, length us, event | category | flops | bytes accessed | tf_op | source)
XLA Modules:
  0.0 20.0 jit_solution(8328743922375987866)
XLA Ops:
  0.0 0.0 copy-start
  0.8 0.1 broadcast_in_dim.29
  0.8 0.1 broadcast_in_dim.30
  0.9 0.0 copy-start.1
  0.9 0.0 copy-start.2
  0.9 1.7 %fusion.2 = f32[8,256]{1,0:T(8,128)S(1)} fusion(bf16[1,256,2048]{2,1,0:T(8,128)(2,1)} %param.8, bf16[1,8,2048]{2,1,0:T(8,128)(2,1)} %param.10), kind=kOutput, calls=%fused_computation.4 | convolution fusion | flops 8388608 | bytes 1089536 | tf_op jit(solution)/shard_map/dot_general | solution.py:20
  2.6 0.0 copy-done
  2.6 0.0 copy-done.1
  2.6 0.0 copy-done.2
  2.6 0.8 %convolution_bitcast_fusion = bf16[1,8,8,128]{3,1,2,0:T(8,128)(2,1)S(1)} fusion(bf16[1024,256]{1,0:T(8,128)(2,1)S(1)} %copy-done.1, f32[8,256]{1,0:T(8,128)S(1)} %fusion.2, bf16[1,256,2048]{2,1,0:T(8,128)(2,1)S(1)} %copy-done, bf16[1,8,2048]{2,1,0:T(8,128)(2,1)S(1)} %copy-done.2), kind=kOutput, calls=%fused_computation | convolution fusion | flops 12587008 | bytes 1630208 | tf_op jit(solution)/shard_map/dot_general | solution.py:26
  3.6 0.7 %select_convert_fusion = bf16[32,8,128]{2,1,0:T(8,128)(2,1)} fusion(bf16[32,8,128]{2,1,0:T(8,128)(2,1)S(1)} %bitcast.32, pred[8]{0:T(512)(128)(4,1)S(1)} %broadcast_in_dim.30), kind=kLoop, calls=%fused_computation.8 | loop fusion | flops 32768 | bytes 131080 | tf_op jit(solution)/shard_map/convert_element_type | solution.py:34
  4.3 0.0 copy-start.3
  4.3 7.3 %all-to-all-start = ((bf16[32,8,128]{2,1,0:T(8,128)(2,1)}), bf16[32,8,128]{2,1,0:T(8,128)(2,1)S(1)}, u32[]{:S(2)}, u32[]{:S(2)}) async-start(bf16[32,8,128]{2,1,0:T(8,128)(2,1)} %select_convert_fusion), calls=%async_computation | async-start | bytes 131072 | tf_op jit(solution)/shard_map/all_to_all | solution.py:36
  11.6 0.0 copy-done.3
  11.6 7.2 %all-to-all-done = bf16[32,8,128]{2,1,0:T(8,128)(2,1)S(1)} async-done(((bf16[32,8,128]{2,1,0:T(8,128)(2,1)}), bf16[32,8,128]{2,1,0:T(8,128)(2,1)S(1)}, u32[]{:S(2)}, u32[]{:S(2)}) %all-to-all-start) | async-done | bytes 65568 | tf_op jit(solution)/shard_map/all_to_all | solution.py:36
  18.9 1.0 %add_convert_fusion = bf16[2,512,128]{2,1,0:T(8,128)(2,1)} fusion(f32[2,128]{1,0:T(2,128)S(1)} %get-tuple-element.10, f32[512]{0:T(512)S(1)} %bitcast.37, f32[2,128]{1,0:T(2,128)S(1)} %get-tuple-element.11, f32[512]{0:T(512)S(1)} %bitcast.38, f32[2,128]{1,0:T(2,128)S(1)} %get-tuple-element.12, f32[512]{0:T(512)S(1)} %bitcast.36, ...), kind=kLoop, calls=%fused_computation.6 | loop fusion | flops 1048576 | bytes 274432 | tf_op jit(solution)/shard_map/convert_element_type | solution.py:41
  (8 shorter events, 0.1 us)
Async XLA Ops:
  0.0 2.6 %copy-start = (bf16[1,256,2048]{2,1,0:T(8,128)(2,1)S(1)}, bf16[1,256,2048]{2,1,0:T(8,128)(2,1)}, u32[]{:S(2)}) copy-start(bf16[1,256,2048]{2,1,0:T(8,128)(2,1)} %param.9) | copy-start | bytes 3145732
  0.9 1.7 %copy-start.1 = (bf16[1024,256]{1,0:T(8,128)(2,1)S(1)}, bf16[1024,256]{1,0:T(8,128)(2,1)}, u32[]{:S(2)}) copy-start(bf16[1024,256]{1,0:T(8,128)(2,1)} %param.12) | copy-start | bytes 1572868
  0.9 1.7 %copy-start.2 = (bf16[1,8,2048]{2,1,0:T(8,128)(2,1)S(1)}, bf16[1,8,2048]{2,1,0:T(8,128)(2,1)}, u32[]{:S(2)}) copy-start(bf16[1,8,2048]{2,1,0:T(8,128)(2,1)} %param.11) | copy-start | bytes 98308
  4.3 7.3 %copy-start.3 = (f32[512,4]{0,1:T(4,128)S(1)}, f32[512,4]{0,1:T(4,128)}, u32[]{:S(2)}) copy-start(f32[512,4]{0,1:T(4,128)} %param.13) | copy-start | bytes 24580
  4.3 14.6 %all-to-all-start = ((bf16[32,8,128]{2,1,0:T(8,128)(2,1)}), bf16[32,8,128]{2,1,0:T(8,128)(2,1)S(1)}, u32[]{:S(2)}, u32[]{:S(2)}) async-start(bf16[32,8,128]{2,1,0:T(8,128)(2,1)} %select_convert_fusion), calls=%async_computation | async-start | bytes 131072 | tf_op jit(solution)/shard_map/all_to_all | solution.py:36

commit v2 on v1

v2 whole, which is shorter than its diff:
```python
import functools

import jax
import jax.numpy as jnp
from jax import lax
from jax.experimental import pallas as pl
from jax.experimental.pallas import tpu as pltpu
from jax.sharding import PartitionSpec as P

ROWS = (((1,), (1,)), ((), ()))


def fetch(index_ref, aux_hbm, dressed_hbm, coefs_hbm, levels_hbm,
          aux_ref, dressed_ref, coefs_ref, mask_ref, wide_ref, levels_ref, sems, *, q_own):
    moves = (
        (levels_hbm, levels_ref),
        (aux_hbm, aux_ref),
        (dressed_hbm, dressed_ref),
        (coefs_hbm, coefs_ref),
    )
    copies = [
        pltpu.make_async_copy(source, target, sems.at[k]) for k, (source, target) in enumerate(moves)
    ]
    for copy in copies:
        copy.start()
    slot = lax.broadcasted_iota(jnp.int32, mask_ref.shape, 0)
    mask_ref[...] = (slot // q_own == index_ref[0]).astype(jnp.float32)
    copies[0].wait()
    coefs = jnp.transpose(levels_ref[...])
    for i in range(wide_ref.shape[0]):
        wide_ref[i] = jnp.broadcast_to(coefs[:, i : i + 1], wide_ref.shape[1:])
    for copy in copies[1:]:
        copy.wait()


def before(mask_ref, product_ref, coefs_ref, cells_ref, *, levels):
    cells, slots, nu_own = cells_ref.shape
    q_own = slots // levels
    pairs = product_ref.shape[0] // q_own
    blocks = cells // pairs
    product = product_ref[...]
    mine = mask_ref[:, 0:1] > 0.5
    placed = [
        jnp.where(mine, jnp.concatenate([product[p * q_own : (p + 1) * q_own]] * levels, axis=0), 0.0)
        for p in range(pairs)
    ]
    placed = jnp.concatenate(placed, axis=0).astype(jnp.bfloat16)
    half = lax.dot_general(placed, coefs_ref[...], ROWS, preferred_element_type=jnp.float32)
    half = half.astype(jnp.bfloat16)
    for p in range(pairs):
        for x in range(blocks):
            cells_ref[p * blocks + x] = half[
                p * slots : (p + 1) * slots, x * nu_own : (x + 1) * nu_own
            ]


def after(cells_ref, wide_ref, out_hbm, out_ref, sems, *, levels):
    q_own = out_ref.shape[0]
    summed = cells_ref[...].astype(jnp.float32).sum(axis=0)
    copies = []
    for q in range(q_own):
        total = wide_ref[0] * summed[q : q + 1]
        for i in range(1, levels):
            total = total + wide_ref[i] * summed[i * q_own + q : i * q_own + q + 1]
        out_ref[q] = total.astype(out_ref.dtype)
        copies.append(pltpu.make_async_copy(out_ref.at[q], out_hbm.at[q], sems.at[q]))
        copies[-1].start()
    for copy in copies:
        copy.wait()


def shards(
    occupied_index,
    doubles_slab,
    lambda_slab,
    aux_factors,
    dressed_factors,
    virtual_coefs,
    occupied_coefs,
):
    pairs = lax.axis_size("pair")
    blocks = lax.axis_size("aux")
    mu, levels = occupied_coefs.shape
    q_own = aux_factors.shape[1] // pairs
    nu_own = virtual_coefs.shape[0] // blocks
    limit = (4 << 20) + 16 * pairs * blocks * levels * q_own * nu_own
    vmem = pl.BlockSpec(memory_space=pltpu.VMEM)
    hbm = pl.BlockSpec(memory_space=pl.ANY)
    fetched = (aux_factors, dressed_factors, virtual_coefs, occupied_coefs.T)
    aux_factors, dressed_factors, virtual_coefs, mask, wide = pl.pallas_call(
        functools.partial(fetch, q_own=q_own),
        out_shape=tuple(pltpu.VMEM(x.shape, x.dtype) for x in fetched[:3])
        + (
            pltpu.VMEM((levels * q_own, 128), jnp.float32),
            pltpu.VMEM((levels, mu, nu_own), jnp.float32),
        ),
        in_specs=[pl.BlockSpec(memory_space=pltpu.SMEM)] + [hbm] * 4,
        out_specs=(vmem,) * 5,
        scratch_shapes=[
            pltpu.VMEM((levels, mu), jnp.float32),
            pltpu.SemaphoreType.DMA((4,)),
        ],
        name="fetch",
        compiler_params=pltpu.CompilerParams(vmem_limit_bytes=limit),
    )(occupied_index, *(pltpu.with_memory_space_constraint(x, pltpu.HBM) for x in fetched))
    product = lax.dot_general(
        aux_factors[0], doubles_slab[0], ROWS, preferred_element_type=jnp.float32
    )
    product = product + lax.dot_general(
        dressed_factors[0], lambda_slab[0], ROWS, preferred_element_type=jnp.float32
    )
    inputs = [
        pltpu.with_memory_space_constraint(x, pltpu.VMEM)
        for x in (mask, product, virtual_coefs)
    ]
    cells = pl.pallas_call(
        functools.partial(before, levels=levels),
        out_shape=pltpu.VMEM((pairs * blocks, levels * q_own, nu_own), jnp.bfloat16),
        in_specs=[vmem] * 3,
        out_specs=vmem,
        name="before",
        compiler_params=pltpu.CompilerParams(vmem_limit_bytes=limit),
    )(*inputs)
    received = lax.all_to_all(cells, ("pair", "aux"), split_axis=0, concat_axis=0, tiled=True)
    received = pltpu.with_memory_space_constraint(received, pltpu.VMEM)
    wide = pltpu.with_memory_space_constraint(wide, pltpu.VMEM)
    return pl.pallas_call(
        functools.partial(after, levels=levels),
        out_shape=jax.ShapeDtypeStruct((q_own, mu, nu_own), jnp.bfloat16),
        in_specs=[vmem, vmem],
        out_specs=hbm,
        scratch_shapes=[
            pltpu.VMEM((q_own, mu, nu_own), jnp.bfloat16),
            pltpu.SemaphoreType.DMA((q_own,)),
        ],
        name="after",
        compiler_params=pltpu.CompilerParams(vmem_limit_bytes=limit),
    )(received, wide)


def solution(mesh):
    placed = (
        P("pair"),
        P("pair", "aux", None),
        P("pair", "aux", None),
        P("pair", None, None),
        P("pair", None, None),
        P(None, "aux"),
        P(),
    )
    return jax.shard_map(
        shards, mesh=mesh, in_specs=placed, out_specs=P("pair", None, "aux"), check_vma=False
    )
```

time: 20.2 us -> 18.5 us (0.916)
  blocking collectives: 0 us -> 14.4 us
  starting transfers between devices: 7.33 us -> 0 us
  waiting for transfers between devices: 7.25 us -> 0 us
  Pallas kernels: 0 us -> 2.28 us
  other arithmetic: 1.8 us -> 0 us
  matrix products: 2.48 us -> 0.76 us
  local copies, waits for them, and re-layouts: 0.29 us -> 0.01 us
    all_to_all x0 -> x1, blocking collectives: none -> 14.4 us  [shards(): lax.all_to_all(cells, ('pair', 'aux'), split_axis=0, concat_axis=0, tiled...]
    all_to_all x1 -> x0, starting transfers between devices: 7.33 us -> none  [shards(): lax.all_to_all(cells, ('pair', 'aux'), split_axis=0, concat_axis=0, tiled...]
    all_to_all x1 -> x0, waiting for transfers between devices: 7.25 us -> none  [shards(): lax.all_to_all(cells, ('pair', 'aux'), split_axis=0, concat_axis=0, tiled...]
    pallas_call x0 -> x3, Pallas kernels: none -> 2.28 us  [the longest x1 1.2 us: shards(): pl.pallas_call(functools.partial(fetch, q_own=q_own), out_shape=tuple((pl...]
    convert_element_type x2 -> x0, other arithmetic: 1.75 us -> none  [the longest x1 1.04 us: shards(): return gamma_basis.astype(jnp.bfloat16)]
    dot_general x2, matrix products: 2.48 us -> 0.76 us  [the longest x1 0.39 us: shards(): lax.dot_general(dressed_factors[0], lambda_slab[0], ROWS, preferred_eleme...]
    broadcast_in_dim x4 -> x0, local copies, waits for them, and re-layouts: 0.22 us -> none  [shards(): jnp.where(mine[None, :, None, None], cells, 0.0).astype(jnp.bfloat16)]
  transfers between devices with their start and end apart: 1 -> 0, of which waited for: 1 -> 0; matrix products, arithmetic and copies ran while one was open for 0% -> 0% of each run, Pallas kernels for 0% -> 0%
where the time goes in v2:
time: 18.5 us; the launch traced here: 18.3 us
  blocking collectives  14.4 us (78%)
  Pallas kernels  2.28 us (12%)
  between operations  0.82 us (4%)
  matrix products  0.76 us (4%)
    all_to_all x1, blocking collectives, shards(): lax.all_to_all(cells, ('pair', 'aux'), split_axis=0, concat_axis=0, tiled...  14.4 us
    pallas_call x1, Pallas kernels, shards(): pl.pallas_call(functools.partial(fetch, q_own=q_own), out_shape=tuple((pl...  1.2 us
    pallas_call x1, Pallas kernels, shards(): pl.pallas_call(functools.partial(after, levels=levels), out_shape=jax.Sha...  0.84 us
    dot_general x1, matrix products, shards(): lax.dot_general(dressed_factors[0], lambda_slab[0], ROWS, preferred_eleme...  0.39 us
    dot_general x1, matrix products, shards(): lax.dot_general(aux_factors[0], doubles_slab[0], ROWS, preferred_element_...  0.37 us

profile of v2, /device:TPU:0, one launch (start us, length us, event | category | flops | bytes accessed | tf_op | source)
XLA Modules:
  0.0 18.3 jit_solution(12261312726011654537)
XLA Ops:
  0.0 0.0 copy-start
  0.0 0.0 copy-start.1
  0.8 1.2 %fetch.1 = (bf16[1,8,2048]{2,1,0:T(8,128)(2,1)S(1)}, bf16[1,8,2048]{2,1,0:T(8,128)(2,1)S(1)}, bf16[1024,256]{1,0:T(8,128)(2,1)S(1)}, f32[8,128]{1,0:T(8,128)S(1)}, f32[4,512,128]{2,1,0:T(8,128)S(1)}) custom-call(s32[1]{0:T(128)S(6)} %copy.8.index_ref, bf16[1,8,2048]{2,1,0:T(8,128)(2,1)} %aux_hbm.1, bf16[1,8,2048]{2,1,0:T(8,128)(2,1)} %dressed_hbm.1, ...), custom_call_target="tpu_custom_call" | custom-call | tf_op jit(solution)/shard_map/fetch/pallas_call | solution.py:90
  2.0 0.0 copy-done
  2.0 0.4 %fusion.1 = f32[8,256]{1,0:T(8,128)S(1)} fusion(bf16[1,256,2048]{2,1,0:T(8,128)(2,1)S(1)} %copy-done, bf16[1,8,2048]{2,1,0:T(8,128)(2,1)S(1)} %get-tuple-element.11), kind=kOutput, calls=%fused_computation.2 | convolution fusion | flops 8388608 | bytes 1089536 | tf_op jit(solution)/shard_map/dot_general | solution.py:106
  2.4 0.0 copy-done.1
  2.4 0.4 %convolution_add_fusion.product_ref = f32[8,256]{1,0:T(8,128)S(1)} fusion(f32[8,256]{1,0:T(8,128)S(1)} %fusion.1, bf16[1,256,2048]{2,1,0:T(8,128)(2,1)S(1)} %copy-done.1, bf16[1,8,2048]{2,1,0:T(8,128)(2,1)S(1)} %get-tuple-element.12), kind=kOutput, calls=%fused_computation | convolution fusion | flops 8390656 | bytes 1097728 | tf_op jit(solution)/shard_map/dot_general | solution.py:109
  2.8 0.2 %before.1 = bf16[32,8,128]{2,1,0:T(8,128)(2,1)S(1)} custom-call(f32[8,128]{1,0:T(8,128)S(1)} %get-tuple-element.10.mask_ref, f32[8,256]{1,0:T(8,128)S(1)} %convolution_add_fusion.product_ref, bf16[1024,256]{1,0:T(8,128)(2,1)S(1)} %get-tuple-element.13.coefs_ref), custom_call_target="tpu_custom_call" | custom-call | tf_op jit(solution)/shard_map/before/pallas_call | solution.py:116
  3.0 14.4 %all_to_all.5.cells_ref = bf16[32,8,128]{2,1,0:T(8,128)(2,1)S(1)} all-to-all(bf16[32,8,128]{2,1,0:T(8,128)(2,1)S(1)} %before.1), channel_id=1, replica_groups=mesh['pair'=4,'aux'=8] {'pair','aux'}, dimensions={0} | all-to-all | bytes 131072 | tf_op jit(solution)/shard_map/all_to_all | solution.py:124
  17.5 0.8 %after.1 = bf16[2,512,128]{2,1,0:T(8,128)(2,1)} custom-call(bf16[32,8,128]{2,1,0:T(8,128)(2,1)S(1)} %all_to_all.5.cells_ref, f32[4,512,128]{2,1,0:T(8,128)S(1)} %get-tuple-element.14.wide_ref), custom_call_target="tpu_custom_call" | custom-call | tf_op jit(solution)/shard_map/after/pallas_call | solution.py:127
Async XLA Ops:
  0.0 2.0 %copy-start = (bf16[1,256,2048]{2,1,0:T(8,128)(2,1)S(1)}, bf16[1,256,2048]{2,1,0:T(8,128)(2,1)}, u32[]{:S(2)}) copy-start(bf16[1,256,2048]{2,1,0:T(8,128)(2,1)} %param.8) | copy-start | bytes 3145732
  0.0 2.4 %copy-start.1 = (bf16[1,256,2048]{2,1,0:T(8,128)(2,1)S(1)}, bf16[1,256,2048]{2,1,0:T(8,128)(2,1)}, u32[]{:S(2)}) copy-start(bf16[1,256,2048]{2,1,0:T(8,128)(2,1)} %param.9) | copy-start | bytes 3145732

commit v3 on v2

v3 whole, which is shorter than its diff:
```python
import functools

import jax
import jax.numpy as jnp
from jax import lax
from jax.experimental import pallas as pl
from jax.experimental.pallas import tpu as pltpu
from jax.sharding import PartitionSpec as P

FLOPS = 1 << 33
ROWS = (((1,), (1,)), ((), ()))


def level(row_ref, *, q_own):
    row_ref[...] = (lax.broadcasted_iota(jnp.int32, row_ref.shape, 0) // q_own).astype(jnp.float32)


def widen(coefs_ref, wide_ref, tag_ref):
    tag_ref[...] = jnp.zeros(tag_ref.shape, tag_ref.dtype)
    coefs = jnp.transpose(coefs_ref[...])
    for i in range(wide_ref.shape[0]):
        wide_ref[i] = jnp.broadcast_to(coefs[:, i : i + 1], wide_ref.shape[1:])


def first(aux_ref, dressed_ref, tag_ref, doubles_ref, product_ref):
    product_ref[...] = lax.dot_general(
        aux_ref[0], doubles_ref[0], ROWS, preferred_element_type=jnp.float32
    )


def before(index_ref, rows_ref, product_ref, dressed_ref, lambda_ref, coefs_ref, cells_ref, *, levels):
    cells, slots, nu_own = cells_ref.shape
    q_own = slots // levels
    pairs = product_ref.shape[0] // q_own
    blocks = cells // pairs
    product = product_ref[...] + lax.dot_general(
        dressed_ref[0], lambda_ref[0], ROWS, preferred_element_type=jnp.float32
    )
    mine = rows_ref[:, 0:1] == index_ref[0].astype(jnp.float32)
    placed = [
        jnp.where(mine, jnp.concatenate([product[p * q_own : (p + 1) * q_own]] * levels, axis=0), 0.0)
        for p in range(pairs)
    ]
    placed = jnp.concatenate(placed, axis=0).astype(jnp.bfloat16)
    half = lax.dot_general(placed, coefs_ref[...], ROWS, preferred_element_type=jnp.float32)
    half = half.astype(jnp.bfloat16)
    for p in range(pairs):
        for x in range(blocks):
            cells_ref[p * blocks + x] = half[
                p * slots : (p + 1) * slots, x * nu_own : (x + 1) * nu_own
            ]


def after(cells_ref, wide_ref, out_hbm, out_ref, sems, *, levels):
    q_own = out_ref.shape[0]
    summed = cells_ref[...].astype(jnp.float32).sum(axis=0)
    copies = []
    for q in range(q_own):
        total = wide_ref[0] * summed[q : q + 1]
        for i in range(1, levels):
            total = total + wide_ref[i] * summed[i * q_own + q : i * q_own + q + 1]
        out_ref[q] = total.astype(out_ref.dtype)
        copies.append(pltpu.make_async_copy(out_ref.at[q], out_hbm.at[q], sems.at[q]))
        copies[-1].start()
    for copy in copies:
        copy.wait()


def shards(
    occupied_index,
    doubles_slab,
    lambda_slab,
    aux_factors,
    dressed_factors,
    virtual_coefs,
    occupied_coefs,
):
    pairs = lax.axis_size("pair")
    blocks = lax.axis_size("aux")
    mu, levels = occupied_coefs.shape
    q_own = aux_factors.shape[1] // pairs
    nu_own = virtual_coefs.shape[0] // blocks
    limit = (4 << 20) + 16 * pairs * blocks * levels * q_own * nu_own
    vmem = pl.BlockSpec(memory_space=pltpu.VMEM)
    hbm = pl.BlockSpec(memory_space=pl.ANY)
    pin = lambda *xs: [pltpu.with_memory_space_constraint(x, pltpu.VMEM) for x in xs]
    params = pltpu.CompilerParams(vmem_limit_bytes=limit)
    (dressed_factors,) = pin(dressed_factors)
    rows = pl.pallas_call(
        functools.partial(level, q_own=q_own),
        out_shape=pltpu.VMEM((levels * q_own, 128), jnp.float32),
        in_specs=[],
        out_specs=vmem,
        name="level",
        compiler_params=params,
        cost_estimate=pl.CostEstimate(flops=FLOPS, transcendentals=0, bytes_accessed=0),
    )()
    wide, tag = pl.pallas_call(
        widen,
        out_shape=(
            pltpu.VMEM((levels, mu, nu_own), jnp.float32),
            pltpu.VMEM((8, 128), jnp.float32),
        ),
        in_specs=[vmem],
        out_specs=(vmem, vmem),
        name="widen",
        compiler_params=params,
        cost_estimate=pl.CostEstimate(flops=1, transcendentals=0, bytes_accessed=1),
    )(*pin(occupied_coefs.T))
    wide, tag = pin(wide, tag)
    product = pl.pallas_call(
        first,
        out_shape=pltpu.VMEM((aux_factors.shape[1], doubles_slab.shape[1]), jnp.float32),
        in_specs=[vmem] * 4,
        out_specs=vmem,
        name="first",
        compiler_params=params,
        cost_estimate=pl.CostEstimate(flops=1, transcendentals=0, bytes_accessed=1),
    )(*pin(aux_factors), dressed_factors, tag, *pin(doubles_slab))
    cells = pl.pallas_call(
        functools.partial(before, levels=levels),
        out_shape=pltpu.VMEM((pairs * blocks, levels * q_own, nu_own), jnp.bfloat16),
        in_specs=[pl.BlockSpec(memory_space=pltpu.SMEM)] + [vmem] * 5,
        out_specs=vmem,
        name="before",
        compiler_params=params,
    )(occupied_index, *pin(rows, product), dressed_factors, *pin(lambda_slab, virtual_coefs))
    received = lax.all_to_all(cells, ("pair", "aux"), split_axis=0, concat_axis=0, tiled=True)
    return pl.pallas_call(
        functools.partial(after, levels=levels),
        out_shape=jax.ShapeDtypeStruct((q_own, mu, nu_own), jnp.bfloat16),
        in_specs=[vmem, vmem],
        out_specs=hbm,
        scratch_shapes=[
            pltpu.VMEM((q_own, mu, nu_own), jnp.bfloat16),
            pltpu.SemaphoreType.DMA((q_own,)),
        ],
        name="after",
        compiler_params=params,
    )(*pin(received), wide)


def solution(mesh):
    placed = (
        P("pair"),
        P("pair", "aux", None),
        P("pair", "aux", None),
        P("pair", None, None),
        P("pair", None, None),
        P(None, "aux"),
        P(),
    )
    return jax.shard_map(
        shards, mesh=mesh, in_specs=placed, out_specs=P("pair", None, "aux"), check_vma=False
    )
```

time: 18.5 us -> 17.8 us (0.962)
  matrix products: 0.76 us -> 0 us
    dot_general x2 -> x0, matrix products: 0.76 us -> none  [the longest x1 0.39 us: shards(): lax.dot_general(dressed_factors[0], lambda_slab[0], ROWS, preferred_eleme...]
    pallas_call x1 -> x3, Pallas kernels: 1.2 us -> 0.84 us  [the longest x1 0.46 us: shards(): pl.pallas_call(widen, out_shape=(pltpu.VMEM((levels, mu, nu_own), jnp.flo...]
    pallas_call x1, Pallas kernels: 0.25 us -> 0.55 us  [shards(): pl.pallas_call(functools.partial(before, levels=levels), out_shape=pltpu....]
where the time goes in v3:
time: 17.8 us; the launch traced here: 17.6 us
  blocking collectives  14.4 us (81%)
  Pallas kernels  2.22 us (12%)
  between operations  0.85 us (5%)
    all_to_all x1, blocking collectives, shards(): lax.all_to_all(cells, ('pair', 'aux'), split_axis=0, concat_axis=0, tiled...  14.4 us
    pallas_call x1, Pallas kernels, shards(): pl.pallas_call(functools.partial(after, levels=levels), out_shape=jax.Sha...  0.84 us
    pallas_call x1, Pallas kernels, shards(): pl.pallas_call(functools.partial(before, levels=levels), out_shape=pltpu....  0.55 us
    pallas_call x1, Pallas kernels, shards(): pl.pallas_call(widen, out_shape=(pltpu.VMEM((levels, mu, nu_own), jnp.flo...  0.46 us
    pallas_call x1, Pallas kernels, shards(): pl.pallas_call(first, out_shape=pltpu.VMEM((aux_factors.shape[1], doubles...  0.37 us

profile of v3, /device:TPU:0, one launch (start us, length us, event | category | flops | bytes accessed | tf_op | source)
XLA Modules:
  0.0 17.6 jit_solution(2685212609299564794)
XLA Ops:
  0.0 0.0 copy-start.1
  0.0 0.0 copy-start.5
  0.0 0.0 copy-start.3
  0.0 0.0 copy-start.4
  0.0 0.0 copy-start.2
  0.0 0.0 copy-start
  0.8 0.0 copy-done.5
  0.8 0.5 %widen.1 = (f32[4,512,128]{2,1,0:T(8,128)S(1)}, f32[8,128]{1,0:T(8,128)S(1)}) custom-call(f32[4,512]{1,0:T(4,128)S(1)} %bitcast.1), custom_call_target="tpu_custom_call" | custom-call | flops 1 | bytes 1 | tf_op jit(solution)/shard_map/widen/pallas_call | solution.py:98
  1.3 0.0 copy-done.1
  1.3 0.0 copy-done.3
  1.3 0.0 copy-done.4
  1.3 0.4 %first.1.product_ref = f32[8,256]{1,0:T(8,128)S(1)} custom-call(bf16[1,8,2048]{2,1,0:T(8,128)(2,1)S(1)} %copy-done.4, bf16[1,8,2048]{2,1,0:T(8,128)(2,1)S(1)} %copy-done.3, f32[8,128]{1,0:T(8,128)S(1)} %get-tuple-element.7.tag_ref, bf16[1,256,2048]{2,1,0:T(8,128)(2,1)S(1)} %copy-done.1), custom_call_target="tpu_custom_call" | custom-call | flops 1 | bytes 1 | tf_op jit(solution)/shard_map/first/pallas_call | solution.py:111
  1.7 0.0 copy-done.2
  1.7 0.1 copy-done
  1.8 0.6 %before.1 = bf16[32,8,128]{2,1,0:T(8,128)(2,1)S(1)} custom-call(s32[1]{0:T(128)S(6)} %copy.8.index_ref, f32[8,128]{1,0:T(8,128)S(1)} %level.1.rows_ref, f32[8,256]{1,0:T(8,128)S(1)} %first.1.product_ref, bf16[1,8,2048]{2,1,0:T(8,128)(2,1)S(1)} %copy-done.3, bf16[1,256,2048]{2,1,0:T(8,128)(2,1)S(1)} %copy-done, bf16[1024,256]{1,0:T(8,128)(2,1)S(1)} %copy-done.2), custom_call_target="tpu_custom_call" | custom-call | tf_op jit(solution)/shard_map/before/pallas_call | solution.py:120
  2.3 14.4 %all_to_all.5.cells_ref = bf16[32,8,128]{2,1,0:T(8,128)(2,1)S(1)} all-to-all(bf16[32,8,128]{2,1,0:T(8,128)(2,1)S(1)} %before.1), channel_id=1, replica_groups=mesh['pair'=4,'aux'=8] {'pair','aux'}, dimensions={0} | all-to-all | bytes 131072 | tf_op jit(solution)/shard_map/all_to_all | solution.py:128
  16.8 0.8 %after.1 = bf16[2,512,128]{2,1,0:T(8,128)(2,1)} custom-call(bf16[32,8,128]{2,1,0:T(8,128)(2,1)S(1)} %all_to_all.5.cells_ref, f32[4,512,128]{2,1,0:T(8,128)S(1)} %get-tuple-element.8.wide_ref), custom_call_target="tpu_custom_call" | custom-call | tf_op jit(solution)/shard_map/after/pallas_call | solution.py:129
  (1 shorter events, 0.0 us)
Async XLA Ops:
  0.0 1.3 %copy-start.1 = (bf16[1,256,2048]{2,1,0:T(8,128)(2,1)S(1)}, bf16[1,256,2048]{2,1,0:T(8,128)(2,1)}, u32[]{:S(2)}) copy-start(bf16[1,256,2048]{2,1,0:T(8,128)(2,1)} %doubles_ref.1) | copy-start | bytes 3145732
  0.0 0.8 %copy-start.5 = (f32[512,4]{0,1:T(4,128)S(1)}, f32[512,4]{0,1:T(4,128)}, u32[]{:S(2)}) copy-start(f32[512,4]{0,1:T(4,128)} %param.13) | copy-start | bytes 24580
  0.0 1.3 %copy-start.3 = (bf16[1,8,2048]{2,1,0:T(8,128)(2,1)S(1)}, bf16[1,8,2048]{2,1,0:T(8,128)(2,1)}, u32[]{:S(2)}) copy-start(bf16[1,8,2048]{2,1,0:T(8,128)(2,1)} %dressed_ref.3) | copy-start | bytes 98308
  0.0 1.3 %copy-start.4 = (bf16[1,8,2048]{2,1,0:T(8,128)(2,1)S(1)}, bf16[1,8,2048]{2,1,0:T(8,128)(2,1)}, u32[]{:S(2)}) copy-start(bf16[1,8,2048]{2,1,0:T(8,128)(2,1)} %aux_ref.1) | copy-start | bytes 98308
  0.0 1.7 %copy-start.2 = (bf16[1024,256]{1,0:T(8,128)(2,1)S(1)}, bf16[1024,256]{1,0:T(8,128)(2,1)}, u32[]{:S(2)}) copy-start(bf16[1024,256]{1,0:T(8,128)(2,1)} %coefs_ref.1) | copy-start | bytes 1572868
  0.0 1.7 %copy-start = (bf16[1,256,2048]{2,1,0:T(8,128)(2,1)S(1)}, bf16[1,256,2048]{2,1,0:T(8,128)(2,1)}, u32[]{:S(2)}) copy-start(bf16[1,256,2048]{2,1,0:T(8,128)(2,1)} %lambda_ref.1) | copy-start | bytes 3145732

commit v4 on v3

--- a/solution.py
+++ b/solution.py
@@ -15,8 +15,8 @@
     row_ref[...] = (lax.broadcasted_iota(jnp.int32, row_ref.shape, 0) // q_own).astype(jnp.float32)
 
 
-def widen(coefs_ref, wide_ref, tag_ref):
-    tag_ref[...] = jnp.zeros(tag_ref.shape, tag_ref.dtype)
+def widen(rows_ref, coefs_ref, wide_ref, tag_ref):
+    tag_ref[...] = rows_ref[...]
     coefs = jnp.transpose(coefs_ref[...])
     for i in range(wide_ref.shape[0]):
         wide_ref[i] = jnp.broadcast_to(coefs[:, i : i + 1], wide_ref.shape[1:])
@@ -28,37 +28,39 @@
     )
 
 
-def before(index_ref, rows_ref, product_ref, dressed_ref, lambda_ref, coefs_ref, cells_ref, *, levels):
-    cells, slots, nu_own = cells_ref.shape
-    q_own = slots // levels
-    pairs = product_ref.shape[0] // q_own
-    blocks = cells // pairs
+def before(index_ref, product_ref, dressed_ref, lambda_ref, coefs_ref, cells_ref):
+    cells, rows, nu_own = cells_ref.shape
+    q_own = rows // 2
     product = product_ref[...] + lax.dot_general(
         dressed_ref[0], lambda_ref[0], ROWS, preferred_element_type=jnp.float32
     )
-    mine = rows_ref[:, 0:1] == index_ref[0].astype(jnp.float32)
-    placed = [
-        jnp.where(mine, jnp.concatenate([product[p * q_own : (p + 1) * q_own]] * levels, axis=0), 0.0)
-        for p in range(pairs)
-    ]
-    placed = jnp.concatenate(placed, axis=0).astype(jnp.bfloat16)
-    half = lax.dot_general(placed, coefs_ref[...], ROWS, preferred_element_type=jnp.float32)
-    half = half.astype(jnp.bfloat16)
+    pairs = product.shape[0] // q_own
+    blocks = cells // pairs
+    half = lax.dot_general(
+        product.astype(jnp.bfloat16), coefs_ref[...], ROWS, preferred_element_type=jnp.float32
+    )
+    sender = jnp.full((q_own, half.shape[1]), index_ref[0].astype(jnp.float32))
     for p in range(pairs):
+        block = jnp.concatenate([half[p * q_own : (p + 1) * q_own], sender], axis=0)
+        block = block.astype(jnp.bfloat16)
         for x in range(blocks):
-            cells_ref[p * blocks + x] = half[
-                p * slots : (p + 1) * slots, x * nu_own : (x + 1) * nu_own
-            ]
+            cells_ref[p * blocks + x] = block[:, x * nu_own : (x + 1) * nu_own]
 
 
-def after(cells_ref, wide_ref, out_hbm, out_ref, sems, *, levels):
+def after(cells_ref, wide_ref, out_hbm, out_ref, sems, *, levels, pairs):
     q_own = out_ref.shape[0]
-    summed = cells_ref[...].astype(jnp.float32).sum(axis=0)
+    blocks = cells_ref.shape[0] // pairs
+    summed = [0.0] * levels
+    for p in range(pairs):
+        cells = cells_ref[p * blocks : (p + 1) * blocks].astype(jnp.float32)
+        values, sender = cells.sum(axis=0)[:q_own], cells[0, q_own:]
+        for i in range(levels):
+            summed[i] = summed[i] + jnp.where(sender == i, values, 0.0)
     copies = []
     for q in range(q_own):
-        total = wide_ref[0] * summed[q : q + 1]
+        total = wide_ref[0] * summed[0][q : q + 1]
         for i in range(1, levels):
-            total = total + wide_ref[i] * summed[i * q_own + q : i * q_own + q + 1]
+            total = total + wide_ref[i] * summed[i][q : q + 1]
         out_ref[q] = total.astype(out_ref.dtype)
         copies.append(pltpu.make_async_copy(out_ref.at[q], out_hbm.at[q], sems.at[q]))
         copies[-1].start()
@@ -99,14 +101,14 @@
         widen,
         out_shape=(
             pltpu.VMEM((levels, mu, nu_own), jnp.float32),
-            pltpu.VMEM((8, 128), jnp.float32),
+            pltpu.VMEM((levels * q_own, 128), jnp.float32),
         ),
-        in_specs=[vmem],
+        in_specs=[vmem] * 2,
         out_specs=(vmem, vmem),
         name="widen",
         compiler_params=params,
         cost_estimate=pl.CostEstimate(flops=1, transcendentals=0, bytes_accessed=1),
-    )(*pin(occupied_coefs.T))
+    )(*pin(rows, occupied_coefs.T))
     wide, tag = pin(wide, tag)
     product = pl.pallas_call(
         first,
@@ -118,16 +120,16 @@
         cost_estimate=pl.CostEstimate(flops=1, transcendentals=0, bytes_accessed=1),
     )(*pin(aux_factors), dressed_factors, tag, *pin(doubles_slab))
     cells = pl.pallas_call(
-        functools.partial(before, levels=levels),
-        out_shape=pltpu.VMEM((pairs * blocks, levels * q_own, nu_own), jnp.bfloat16),
-        in_specs=[pl.BlockSpec(memory_space=pltpu.SMEM)] + [vmem] * 5,
+        before,
+        out_shape=pltpu.VMEM((pairs * blocks, 2 * q_own, nu_own), jnp.bfloat16),
+        in_specs=[pl.BlockSpec(memory_space=pltpu.SMEM)] + [vmem] * 4,
         out_specs=vmem,
         name="before",
         compiler_params=params,
-    )(occupied_index, *pin(rows, product), dressed_factors, *pin(lambda_slab, virtual_coefs))
+    )(occupied_index, *pin(product), dressed_factors, *pin(lambda_slab, virtual_coefs))
     received = lax.all_to_all(cells, ("pair", "aux"), split_axis=0, concat_axis=0, tiled=True)
     return pl.pallas_call(
-        functools.partial(after, levels=levels),
+        functools.partial(after, levels=levels, pairs=pairs),
         out_shape=jax.ShapeDtypeStruct((q_own, mu, nu_own), jnp.bfloat16),
         in_specs=[vmem, vmem],
         out_specs=hbm,

time: 17.8 us -> 17.7 us (level)
  no operation moved by 1% of the time
where the time goes in v4:
time: 17.7 us; the launch traced here: 17.5 us
  blocking collectives  14.4 us (81%)
  Pallas kernels  2.21 us (12%)
  between operations  0.85 us (5%)
    all_to_all x1, blocking collectives, shards(): lax.all_to_all(cells, ('pair', 'aux'), split_axis=0, concat_axis=0, tiled...  14.4 us
    pallas_call x1, Pallas kernels, shards(): pl.pallas_call(functools.partial(after, levels=levels, pairs=pairs), out_...  0.82 us
    pallas_call x1, Pallas kernels, shards(): pl.pallas_call(before, out_shape=pltpu.VMEM((pairs * blocks, 2 * q_own, n...  0.54 us
    pallas_call x1, Pallas kernels, shards(): pl.pallas_call(widen, out_shape=(pltpu.VMEM((levels, mu, nu_own), jnp.flo...  0.46 us
    pallas_call x1, Pallas kernels, shards(): pl.pallas_call(first, out_shape=pltpu.VMEM((aux_factors.shape[1], doubles...  0.37 us

profile of v4, /device:TPU:0, one launch (start us, length us, event | category | flops | bytes accessed | tf_op | source)
XLA Modules:
  0.0 17.5 jit_solution(3972299021116229784)
XLA Ops:
  0.0 0.0 copy-start.1
  0.0 0.0 copy-start.5
  0.0 0.0 copy-start.3
  0.0 0.0 copy-start.4
  0.0 0.0 copy-start.2
  0.0 0.0 copy-start
  0.8 0.0 copy-done.5
  0.8 0.5 %widen.1 = (f32[4,512,128]{2,1,0:T(8,128)S(1)}, f32[8,128]{1,0:T(8,128)S(1)}) custom-call(f32[8,128]{1,0:T(8,128)S(1)} %level.1.rows_ref, f32[4,512]{1,0:T(4,128)S(1)} %bitcast.1), custom_call_target="tpu_custom_call" | custom-call | flops 1 | bytes 1 | tf_op jit(solution)/shard_map/widen/pallas_call | solution.py:100
  1.3 0.0 copy-done.1
  1.3 0.0 copy-done.3
  1.3 0.0 copy-done.4
  1.3 0.4 %first.1.product_ref = f32[8,256]{1,0:T(8,128)S(1)} custom-call(bf16[1,8,2048]{2,1,0:T(8,128)(2,1)S(1)} %copy-done.4, bf16[1,8,2048]{2,1,0:T(8,128)(2,1)S(1)} %copy-done.3, f32[8,128]{1,0:T(8,128)S(1)} %get-tuple-element.7.tag_ref, bf16[1,256,2048]{2,1,0:T(8,128)(2,1)S(1)} %copy-done.1), custom_call_target="tpu_custom_call" | custom-call | flops 1 | bytes 1 | tf_op jit(solution)/shard_map/first/pallas_call | solution.py:113
  1.7 0.0 copy-done.2
  1.7 0.1 copy-done
  1.8 0.5 %before.1 = bf16[32,4,128]{2,1,0:T(4,128)(2,1)S(1)} custom-call(s32[1]{0:T(128)S(6)} %copy.8.index_ref, f32[8,256]{1,0:T(8,128)S(1)} %first.1.product_ref, bf16[1,8,2048]{2,1,0:T(8,128)(2,1)S(1)} %copy-done.3, bf16[1,256,2048]{2,1,0:T(8,128)(2,1)S(1)} %copy-done, bf16[1024,256]{1,0:T(8,128)(2,1)S(1)} %copy-done.2), custom_call_target="tpu_custom_call" | custom-call | tf_op jit(solution)/shard_map/before/pallas_call | solution.py:122
  2.3 14.4 %all_to_all.5.cells_ref = bf16[32,4,128]{2,1,0:T(4,128)(2,1)S(1)} all-to-all(bf16[32,4,128]{2,1,0:T(4,128)(2,1)S(1)} %before.1), channel_id=1, replica_groups=mesh['pair'=4,'aux'=8] {'pair','aux'}, dimensions={0} | all-to-all | bytes 65536 | tf_op jit(solution)/shard_map/all_to_all | solution.py:130
  16.7 0.8 %after.1 = bf16[2,512,128]{2,1,0:T(8,128)(2,1)} custom-call(bf16[32,4,128]{2,1,0:T(4,128)(2,1)S(1)} %all_to_all.5.cells_ref, f32[4,512,128]{2,1,0:T(8,128)S(1)} %get-tuple-element.8.wide_ref), custom_call_target="tpu_custom_call" | custom-call | tf_op jit(solution)/shard_map/after/pallas_call | solution.py:131
  (1 shorter events, 0.0 us)
Async XLA Ops:
  0.0 1.3 %copy-start.1 = (bf16[1,256,2048]{2,1,0:T(8,128)(2,1)S(1)}, bf16[1,256,2048]{2,1,0:T(8,128)(2,1)}, u32[]{:S(2)}) copy-start(bf16[1,256,2048]{2,1,0:T(8,128)(2,1)} %doubles_ref.1) | copy-start | bytes 3145732
  0.0 0.8 %copy-start.5 = (f32[512,4]{0,1:T(4,128)S(1)}, f32[512,4]{0,1:T(4,128)}, u32[]{:S(2)}) copy-start(f32[512,4]{0,1:T(4,128)} %param.13) | copy-start | bytes 24580
  0.0 1.3 %copy-start.3 = (bf16[1,8,2048]{2,1,0:T(8,128)(2,1)S(1)}, bf16[1,8,2048]{2,1,0:T(8,128)(2,1)}, u32[]{:S(2)}) copy-start(bf16[1,8,2048]{2,1,0:T(8,128)(2,1)} %dressed_ref.3) | copy-start | bytes 98308
  0.0 1.3 %copy-start.4 = (bf16[1,8,2048]{2,1,0:T(8,128)(2,1)S(1)}, bf16[1,8,2048]{2,1,0:T(8,128)(2,1)}, u32[]{:S(2)}) copy-start(bf16[1,8,2048]{2,1,0:T(8,128)(2,1)} %aux_ref.1) | copy-start | bytes 98308
  0.0 1.7 %copy-start.2 = (bf16[1024,256]{1,0:T(8,128)(2,1)S(1)}, bf16[1024,256]{1,0:T(8,128)(2,1)}, u32[]{:S(2)}) copy-start(bf16[1024,256]{1,0:T(8,128)(2,1)} %coefs_ref.1) | copy-start | bytes 1572868
  0.0 1.7 %copy-start = (bf16[1,256,2048]{2,1,0:T(8,128)(2,1)S(1)}, bf16[1,256,2048]{2,1,0:T(8,128)(2,1)}, u32[]{:S(2)}) copy-start(bf16[1,256,2048]{2,1,0:T(8,128)(2,1)} %lambda_ref.1) | copy-start | bytes 3145732

commit v5 on v4

--- a/solution.py
+++ b/solution.py
@@ -15,14 +15,14 @@
     row_ref[...] = (lax.broadcasted_iota(jnp.int32, row_ref.shape, 0) // q_own).astype(jnp.float32)
 
 
-def widen(rows_ref, coefs_ref, wide_ref, tag_ref):
+def widen(rows_ref, aux_ref, dressed_ref, coefs_ref, wide_ref, tag_ref):
     tag_ref[...] = rows_ref[...]
     coefs = jnp.transpose(coefs_ref[...])
     for i in range(wide_ref.shape[0]):
         wide_ref[i] = jnp.broadcast_to(coefs[:, i : i + 1], wide_ref.shape[1:])
 
 
-def first(aux_ref, dressed_ref, tag_ref, doubles_ref, product_ref):
+def first(aux_ref, tag_ref, doubles_ref, product_ref):
     product_ref[...] = lax.dot_general(
         aux_ref[0], doubles_ref[0], ROWS, preferred_element_type=jnp.float32
     )
@@ -87,7 +87,7 @@
     hbm = pl.BlockSpec(memory_space=pl.ANY)
     pin = lambda *xs: [pltpu.with_memory_space_constraint(x, pltpu.VMEM) for x in xs]
     params = pltpu.CompilerParams(vmem_limit_bytes=limit)
-    (dressed_factors,) = pin(dressed_factors)
+    aux_factors, dressed_factors = pin(aux_factors, dressed_factors)
     rows = pl.pallas_call(
         functools.partial(level, q_own=q_own),
         out_shape=pltpu.VMEM((levels * q_own, 128), jnp.float32),
@@ -103,22 +103,22 @@
             pltpu.VMEM((levels, mu, nu_own), jnp.float32),
             pltpu.VMEM((levels * q_own, 128), jnp.float32),
         ),
-        in_specs=[vmem] * 2,
+        in_specs=[vmem] * 4,
         out_specs=(vmem, vmem),
         name="widen",
         compiler_params=params,
         cost_estimate=pl.CostEstimate(flops=1, transcendentals=0, bytes_accessed=1),
-    )(*pin(rows, occupied_coefs.T))
+    )(*pin(rows), aux_factors, dressed_factors, *pin(occupied_coefs.T))
     wide, tag = pin(wide, tag)
     product = pl.pallas_call(
         first,
         out_shape=pltpu.VMEM((aux_factors.shape[1], doubles_slab.shape[1]), jnp.float32),
-        in_specs=[vmem] * 4,
+        in_specs=[vmem] * 3,
         out_specs=vmem,
         name="first",
         compiler_params=params,
         cost_estimate=pl.CostEstimate(flops=1, transcendentals=0, bytes_accessed=1),
-    )(*pin(aux_factors), dressed_factors, tag, *pin(doubles_slab))
+    )(aux_factors, tag, *pin(doubles_slab))
     cells = pl.pallas_call(
         before,
         out_shape=pltpu.VMEM((pairs * blocks, 2 * q_own, nu_own), jnp.bfloat16),

time: 17.7 us -> 17.7 us (level)
  no operation moved by 1% of the time
where the time goes in v5:
time: 17.7 us; the launch traced here: 17.5 us
  blocking collectives  14.3 us (81%)
  Pallas kernels  2.21 us (12%)
  between operations  0.85 us (5%)
    all_to_all x1, blocking collectives, shards(): lax.all_to_all(cells, ('pair', 'aux'), split_axis=0, concat_axis=0, tiled...  14.3 us
    pallas_call x1, Pallas kernels, shards(): pl.pallas_call(functools.partial(after, levels=levels, pairs=pairs), out_...  0.82 us
    pallas_call x1, Pallas kernels, shards(): pl.pallas_call(before, out_shape=pltpu.VMEM((pairs * blocks, 2 * q_own, n...  0.54 us
    pallas_call x1, Pallas kernels, shards(): pl.pallas_call(widen, out_shape=(pltpu.VMEM((levels, mu, nu_own), jnp.flo...  0.46 us
    pallas_call x1, Pallas kernels, shards(): pl.pallas_call(first, out_shape=pltpu.VMEM((aux_factors.shape[1], doubles...  0.37 us

profile of v5, /device:TPU:0, one launch (start us, length us, event | category | flops | bytes accessed | tf_op | source)
XLA Modules:
  0.0 17.5 jit_solution(15564225763666700703)
XLA Ops:
  0.0 0.0 copy-start.4
  0.0 0.0 copy-start.3
  0.0 0.0 copy-start.1
  0.0 0.0 copy-start.5
  0.0 0.0 copy-start.2
  0.0 0.0 copy-start
  0.8 0.0 copy-done.4
  0.8 0.0 copy-done.3
  0.9 0.0 copy-done.5
  0.9 0.5 %widen.1 = (f32[4,512,128]{2,1,0:T(8,128)S(1)}, f32[8,128]{1,0:T(8,128)S(1)}) custom-call(f32[8,128]{1,0:T(8,128)S(1)} %level.1.rows_ref, bf16[1,8,2048]{2,1,0:T(8,128)(2,1)S(1)} %copy-done.3, bf16[1,8,2048]{2,1,0:T(8,128)(2,1)S(1)} %copy-done.4, f32[4,512]{1,0:T(4,128)S(1)} %bitcast.1), custom_call_target="tpu_custom_call" | custom-call | flops 1 | bytes 1 | tf_op jit(solution)/shard_map/widen/pallas_call | solution.py:100
  1.3 0.0 copy-done.1
  1.3 0.4 %first.1.product_ref = f32[8,256]{1,0:T(8,128)S(1)} custom-call(bf16[1,8,2048]{2,1,0:T(8,128)(2,1)S(1)} %copy-done.3, f32[8,128]{1,0:T(8,128)S(1)} %get-tuple-element.7.tag_ref, bf16[1,256,2048]{2,1,0:T(8,128)(2,1)S(1)} %copy-done.1), custom_call_target="tpu_custom_call" | custom-call | flops 1 | bytes 1 | tf_op jit(solution)/shard_map/first/pallas_call | solution.py:113
  1.7 0.0 copy-done.2
  1.7 0.1 copy-done
  1.8 0.5 %before.1 = bf16[32,4,128]{2,1,0:T(4,128)(2,1)S(1)} custom-call(s32[1]{0:T(128)S(6)} %copy.8.index_ref, f32[8,256]{1,0:T(8,128)S(1)} %first.1.product_ref, bf16[1,8,2048]{2,1,0:T(8,128)(2,1)S(1)} %copy-done.4, bf16[1,256,2048]{2,1,0:T(8,128)(2,1)S(1)} %copy-done, bf16[1024,256]{1,0:T(8,128)(2,1)S(1)} %copy-done.2), custom_call_target="tpu_custom_call" | custom-call | tf_op jit(solution)/shard_map/before/pallas_call | solution.py:122
  2.3 14.3 %all_to_all.5.cells_ref = bf16[32,4,128]{2,1,0:T(4,128)(2,1)S(1)} all-to-all(bf16[32,4,128]{2,1,0:T(4,128)(2,1)S(1)} %before.1), channel_id=1, replica_groups=mesh['pair'=4,'aux'=8] {'pair','aux'}, dimensions={0} | all-to-all | bytes 65536 | tf_op jit(solution)/shard_map/all_to_all | solution.py:130
  16.7 0.8 %after.1 = bf16[2,512,128]{2,1,0:T(8,128)(2,1)} custom-call(bf16[32,4,128]{2,1,0:T(4,128)(2,1)S(1)} %all_to_all.5.cells_ref, f32[4,512,128]{2,1,0:T(8,128)S(1)} %get-tuple-element.8.wide_ref), custom_call_target="tpu_custom_call" | custom-call | tf_op jit(solution)/shard_map/after/pallas_call | solution.py:131
  (1 shorter events, 0.0 us)
Async XLA Ops:
  0.0 0.8 %copy-start.4 = (bf16[1,8,2048]{2,1,0:T(8,128)(2,1)S(1)}, bf16[1,8,2048]{2,1,0:T(8,128)(2,1)}, u32[]{:S(2)}) copy-start(bf16[1,8,2048]{2,1,0:T(8,128)(2,1)} %dressed_ref.3) | copy-start | bytes 98308
  0.0 0.8 %copy-start.3 = (bf16[1,8,2048]{2,1,0:T(8,128)(2,1)S(1)}, bf16[1,8,2048]{2,1,0:T(8,128)(2,1)}, u32[]{:S(2)}) copy-start(bf16[1,8,2048]{2,1,0:T(8,128)(2,1)} %aux_ref.3) | copy-start | bytes 98308
  0.0 1.3 %copy-start.1 = (bf16[1,256,2048]{2,1,0:T(8,128)(2,1)S(1)}, bf16[1,256,2048]{2,1,0:T(8,128)(2,1)}, u32[]{:S(2)}) copy-start(bf16[1,256,2048]{2,1,0:T(8,128)(2,1)} %doubles_ref.1) | copy-start | bytes 3145732
  0.0 0.9 %copy-start.5 = (f32[512,4]{0,1:T(4,128)S(1)}, f32[512,4]{0,1:T(4,128)}, u32[]{:S(2)}) copy-start(f32[512,4]{0,1:T(4,128)} %param.13) | copy-start | bytes 24580
  0.0 1.7 %copy-start.2 = (bf16[1024,256]{1,0:T(8,128)(2,1)S(1)}, bf16[1024,256]{1,0:T(8,128)(2,1)}, u32[]{:S(2)}) copy-start(bf16[1024,256]{1,0:T(8,128)(2,1)} %coefs_ref.1) | copy-start | bytes 1572868
  0.0 1.7 %copy-start = (bf16[1,256,2048]{2,1,0:T(8,128)(2,1)S(1)}, bf16[1,256,2048]{2,1,0:T(8,128)(2,1)}, u32[]{:S(2)}) copy-start(bf16[1,256,2048]{2,1,0:T(8,128)(2,1)} %lambda_ref.1) | copy-start | bytes 3145732

commit v6 on v5

--- a/solution.py
+++ b/solution.py
@@ -23,8 +23,12 @@
 
 
 def first(aux_ref, tag_ref, doubles_ref, product_ref):
-    product_ref[...] = lax.dot_general(
-        aux_ref[0], doubles_ref[0], ROWS, preferred_element_type=jnp.float32
+    half = doubles_ref.shape[1] // 2
+    product_ref[:, :half] = lax.dot_general(
+        aux_ref[0], doubles_ref[0, :half], ROWS, preferred_element_type=jnp.float32
+    )
+    product_ref[:, half:] = lax.dot_general(
+        aux_ref[0], doubles_ref[0, half:], ROWS, preferred_element_type=jnp.float32
     )
 
 

time: 17.7 us -> 17.7 us (level)
  no operation moved by 1% of the time
where the time goes in v6:
time: 17.7 us; the launch traced here: 17.5 us
  blocking collectives  14.3 us (81%)
  Pallas kernels  2.21 us (12%)
  between operations  0.85 us (5%)
    all_to_all x1, blocking collectives, shards(): lax.all_to_all(cells, ('pair', 'aux'), split_axis=0, concat_axis=0, tiled...  14.3 us
    pallas_call x1, Pallas kernels, shards(): pl.pallas_call(functools.partial(after, levels=levels, pairs=pairs), out_...  0.82 us
    pallas_call x1, Pallas kernels, shards(): pl.pallas_call(before, out_shape=pltpu.VMEM((pairs * blocks, 2 * q_own, n...  0.54 us
    pallas_call x1, Pallas kernels, shards(): pl.pallas_call(widen, out_shape=(pltpu.VMEM((levels, mu, nu_own), jnp.flo...  0.46 us
    pallas_call x1, Pallas kernels, shards(): pl.pallas_call(first, out_shape=pltpu.VMEM((aux_factors.shape[1], doubles...  0.37 us

profile of v6, /device:TPU:0, one launch (start us, length us, event | category | flops | bytes accessed | tf_op | source)
XLA Modules:
  0.0 17.5 jit_solution(18385068514323228955)
XLA Ops:
  0.0 0.0 copy-start.4
  0.0 0.0 copy-start.3
  0.0 0.0 copy-start.1
  0.0 0.0 copy-start.5
  0.0 0.0 copy-start.2
  0.0 0.0 copy-start
  0.8 0.0 copy-done.4
  0.8 0.0 copy-done.3
  0.9 0.0 copy-done.5
  0.9 0.5 %widen.1 = (f32[4,512,128]{2,1,0:T(8,128)S(1)}, f32[8,128]{1,0:T(8,128)S(1)}) custom-call(f32[8,128]{1,0:T(8,128)S(1)} %level.1.rows_ref, bf16[1,8,2048]{2,1,0:T(8,128)(2,1)S(1)} %copy-done.3, bf16[1,8,2048]{2,1,0:T(8,128)(2,1)S(1)} %copy-done.4, f32[4,512]{1,0:T(4,128)S(1)} %bitcast.1), custom_call_target="tpu_custom_call" | custom-call | flops 1 | bytes 1 | tf_op jit(solution)/shard_map/widen/pallas_call | solution.py:104
  1.3 0.0 copy-done.1
  1.3 0.4 %first.1.product_ref = f32[8,256]{1,0:T(8,128)S(1)} custom-call(bf16[1,8,2048]{2,1,0:T(8,128)(2,1)S(1)} %copy-done.3, f32[8,128]{1,0:T(8,128)S(1)} %get-tuple-element.7.tag_ref, bf16[1,256,2048]{2,1,0:T(8,128)(2,1)S(1)} %copy-done.1), custom_call_target="tpu_custom_call" | custom-call | flops 1 | bytes 1 | tf_op jit(solution)/shard_map/first/pallas_call | solution.py:117
  1.7 0.0 copy-done.2
  1.7 0.1 copy-done
  1.8 0.5 %before.1 = bf16[32,4,128]{2,1,0:T(4,128)(2,1)S(1)} custom-call(s32[1]{0:T(128)S(6)} %copy.8.index_ref, f32[8,256]{1,0:T(8,128)S(1)} %first.1.product_ref, bf16[1,8,2048]{2,1,0:T(8,128)(2,1)S(1)} %copy-done.4, bf16[1,256,2048]{2,1,0:T(8,128)(2,1)S(1)} %copy-done, bf16[1024,256]{1,0:T(8,128)(2,1)S(1)} %copy-done.2), custom_call_target="tpu_custom_call" | custom-call | tf_op jit(solution)/shard_map/before/pallas_call | solution.py:126
  2.3 14.3 %all_to_all.5.cells_ref = bf16[32,4,128]{2,1,0:T(4,128)(2,1)S(1)} all-to-all(bf16[32,4,128]{2,1,0:T(4,128)(2,1)S(1)} %before.1), channel_id=1, replica_groups=mesh['pair'=4,'aux'=8] {'pair','aux'}, dimensions={0} | all-to-all | bytes 65536 | tf_op jit(solution)/shard_map/all_to_all | solution.py:134
  16.7 0.8 %after.1 = bf16[2,512,128]{2,1,0:T(8,128)(2,1)} custom-call(bf16[32,4,128]{2,1,0:T(4,128)(2,1)S(1)} %all_to_all.5.cells_ref, f32[4,512,128]{2,1,0:T(8,128)S(1)} %get-tuple-element.8.wide_ref), custom_call_target="tpu_custom_call" | custom-call | tf_op jit(solution)/shard_map/after/pallas_call | solution.py:135
  (1 shorter events, 0.0 us)
Async XLA Ops:
  0.0 0.8 %copy-start.4 = (bf16[1,8,2048]{2,1,0:T(8,128)(2,1)S(1)}, bf16[1,8,2048]{2,1,0:T(8,128)(2,1)}, u32[]{:S(2)}) copy-start(bf16[1,8,2048]{2,1,0:T(8,128)(2,1)} %dressed_ref.3) | copy-start | bytes 98308
  0.0 0.8 %copy-start.3 = (bf16[1,8,2048]{2,1,0:T(8,128)(2,1)S(1)}, bf16[1,8,2048]{2,1,0:T(8,128)(2,1)}, u32[]{:S(2)}) copy-start(bf16[1,8,2048]{2,1,0:T(8,128)(2,1)} %aux_ref.3) | copy-start | bytes 98308
  0.0 1.3 %copy-start.1 = (bf16[1,256,2048]{2,1,0:T(8,128)(2,1)S(1)}, bf16[1,256,2048]{2,1,0:T(8,128)(2,1)}, u32[]{:S(2)}) copy-start(bf16[1,256,2048]{2,1,0:T(8,128)(2,1)} %doubles_ref.1) | copy-start | bytes 3145732
  0.0 0.9 %copy-start.5 = (f32[512,4]{0,1:T(4,128)S(1)}, f32[512,4]{0,1:T(4,128)}, u32[]{:S(2)}) copy-start(f32[512,4]{0,1:T(4,128)} %param.13) | copy-start | bytes 24580
  0.0 1.7 %copy-start.2 = (bf16[1024,256]{1,0:T(8,128)(2,1)S(1)}, bf16[1024,256]{1,0:T(8,128)(2,1)}, u32[]{:S(2)}) copy-start(bf16[1024,256]{1,0:T(8,128)(2,1)} %coefs_ref.1) | copy-start | bytes 1572868
  0.0 1.7 %copy-start = (bf16[1,256,2048]{2,1,0:T(8,128)(2,1)S(1)}, bf16[1,256,2048]{2,1,0:T(8,128)(2,1)}, u32[]{:S(2)}) copy-start(bf16[1,256,2048]{2,1,0:T(8,128)(2,1)} %lambda_ref.1) | copy-start | bytes 3145732
